TPU v7x, 256 devices: a whole 4x4x8 slice. The times are simulated.
256 devices in a mesh: blk: 128 (over z, x, y), rep: 2 (over core).
Axes of the slice: x: 4, y: 4, z: 8, core: 2. Of those that a mesh axis runs over, the one named last changes fastest.
Arguments:
- points: float32 [128, 3, 8192], P('blk'), may hold values from -6 to 6
- normals: float32 [128, 3, 8192], P('blk'), may hold values from -6 to 6
- src_block: int32 [8, 128, 1, 16], P(None, 'blk', None, 'rep'), may hold values from 0 to 63
- tgt_index: int32 [8, 128, 1, 16, 128], P(None, 'blk', None, 'rep'), may hold values from 0 to 8191
- active: int32 [8, 128, 1], P(None, 'blk'), may hold values from 0 to 16
Outputs:
- diag_hess: float32 [128, 36], P('blk')
- gradient: float32 [128, 6], P('blk')
- pair_hess: float32 [8, 128, 1, 36], P(None, 'blk')
Inputs may be any that keep to these rules, and one draw needn't show every extreme that they name: Slots j with j >= active contribute nothing.
All inputs are finite; a program needn't handle non-finite values.
Results may differ from a plain program's by a relative error of at most 0.00017.
Values sent between devices are 32-bit elements; how exact they have to be, the bound alone decides.
A program may use at most 64 MiB of HBM per device.

v0:
```python
import jax
import jax.numpy as jnp
from jax import lax
from jax.sharding import PartitionSpec as P

NB = 16
BLOCK = 128


def passed_along(block, axis, distance):
    devices = range(lax.axis_size(axis))
    route = [((i - distance) % len(devices), i) for i in devices]
    return lax.ppermute(block, axis, route)


def total_of_pieces(shard, axis):
    pieces = lax.all_gather(shard, axis)
    return pieces.sum(axis=0)


def body(points, normals, src_block, tgt_index, active):
    count = points.shape[0]
    npts = points.shape[2]
    rounds = src_block.shape[0]
    per_rep = src_block.shape[3]
    slots = per_rep * BLOCK
    half_id = lax.axis_index("rep")
    lane_block = jnp.arange(slots, dtype=jnp.int32) // BLOCK + half_id * per_rep
    lanes = jnp.arange(BLOCK, dtype=jnp.int32)
    source_ids = jnp.arange(count, dtype=jnp.int32)
    target_ids = jnp.arange(count, dtype=jnp.int32)
    flat_src = jnp.moveaxis(points, 1, 0).reshape(3, count * npts)
    tile = jnp.concatenate([points, normals], axis=1)

    def round_terms(k, arrived):
        blocks = lax.dynamic_index_in_dim(src_block, k, 0, keepdims=False)
        targets = lax.dynamic_index_in_dim(tgt_index, k, 0, keepdims=False).reshape(
            count, count, slots
        )
        sidx = (
            source_ids[:, None, None, None] * npts + blocks[:, :, :, None] * BLOCK + lanes
        ).reshape(count, count, slots)
        tidx = target_ids[None, :, None] * npts + targets
        p = flat_src[:, sidx]
        flat_tgt = jnp.moveaxis(arrived, 1, 0).reshape(6, count * npts)
        picked = flat_tgt[:, tidx]
        q = picked[:3]
        n = picked[3:]
        limit = lax.dynamic_index_in_dim(active, k, 0, keepdims=False)
        live = (lane_block[None, None, :] < limit[:, :, None]).astype(jnp.float32)
        resid = jnp.sum(n * (p - q), axis=0)
        weight = live / (1.0 + resid * resid)
        jacob = jnp.stack(
            [
                p[1] * n[2] - p[2] * n[1],
                p[2] * n[0] - p[0] * n[2],
                p[0] * n[1] - p[1] * n[0],
                n[0],
                n[1],
                n[2],
            ]
        )
        gram = jnp.einsum(
            "istl,jstl->stij", jacob * weight, jacob, precision=lax.Precision.HIGHEST
        ) / (NB * BLOCK)
        push = jnp.einsum(
            "istl,stl->sti", jacob, weight * resid, precision=lax.Precision.HIGHEST
        ) / (NB * BLOCK)
        return (gram.reshape(count, count, 36), push)

    def advance(current):
        joined = passed_along(current, "blk", 1)
        return joined

    store = jnp.zeros((count, 42), jnp.float32)

    def one_round(k, carry):
        current, pair_out, own_h, own_g, kept = carry
        current = advance(current)
        gram, push = round_terms(k, current)
        pair_out = lax.dynamic_update_index_in_dim(pair_out, gram, k, 0)
        own_h = own_h + gram.sum(1)
        own_g = own_g + push.sum(1)
        remote = jnp.concatenate([gram.sum(0), -push.sum(0)], axis=1)
        kept = passed_along(kept, "blk", 1) + remote
        return (current, pair_out, own_h, own_g, kept)

    start_carry = (
        tile,
        jnp.zeros((rounds, count, count, 36), jnp.float32),
        jnp.zeros((count, 36), jnp.float32),
        jnp.zeros((count, 6), jnp.float32),
        store,
    )
    final = lax.fori_loop(0, rounds, one_round, start_carry)
    pair_out, own_h, own_g, kept = (final[1], final[2], final[3], final[4])
    coming = passed_along(kept, "blk", -rounds)
    own_all = jnp.concatenate([own_h, own_g], axis=1) + coming
    total, pair_total = (total_of_pieces(own_all, "rep"), total_of_pieces(pair_out, "rep"))
    scale = 2.0 * rounds * count
    return (total[:, :36] / scale, total[:, 36:] / scale, pair_total)


def solution(mesh):
    return jax.shard_map(
        body,
        mesh=mesh,
        in_specs=(
            P("blk", None, None),
            P("blk", None, None),
            P(None, "blk", None, "rep"),
            P(None, "blk", None, "rep", None),
            P(None, "blk", None),
        ),
        out_specs=(P("blk", None), P("blk", None), P(None, "blk", None, None)),
        check_vma=False,
    )
```

profile of v0, /device:TPU:1, one launch (start us, length us, event | category | flops | bytes accessed | tf_op | source)
XLA Modules:
  0.0 197.8 jit_solution(17490384602896605404)
XLA Ops:
  0.7 3.4 %copy.18 = f32[1,3,8192]{1,2,0:T(8,128)} copy(f32[1,3,8192]{2,0,1:T(1,128)} %param.7) | data formatting | bytes 196608 | tf_op args[0]
  4.3 176.7 %while.22 = (s32[]{:T(128)}, f32[1,6,8192]{2,0,1:T(1,128)S(1)}, f32[8,1,1,36]{3,2,1,0:T(1,128)S(1)}, f32[1,36]{1,0:T(1,128)S(1)}, f32[1,6]{1,0:T(1,128)S(1)}, /*...) while((s32[]{:T(128)}, f32[1,6,8192]{2,0,1:T(1,128)S(1)}, ...), condition=%wide.region_2.3_spmd.clone, body=%wide.region_0.2_spmd.clone.sunk | while | flops 601357 | bytes 2068545 | solution.py:95
  9.9 5.0 %gather_fusion.1 = f32[1024,3]{1,0:T(8,128)S(1)} fusion(f32[3,8192]{0,1:T(8,128)} %get-tuple-element.399, s32[1024]{0:T(1024)S(1)} %broadcast_clamp_fusion.5), kind=kCustom, calls=%fused_computation.clone.clone.1 | custom fusion | bytes 28672 | tf_op jit(solution)/shard_map/while/body/eval_jaxpr/gather | solution.py:44
  14.9 5.2 %collective-permute-done = f32[1,6,8192]{2,0,1:T(1,128)S(1)} collective-permute-done((f32[1,6,8192]{2,0,1:T(1,128)S(1)}, f32[1,6,8192]{2,0,1:T(1,128)S(1)}, u32[]{:S(2)}, u32[]{:S(2)}) %collective-permute-start) | collective-permute-done | bytes 196640 | tf_op jit(solution)/shard_map/while/body/eval_jaxpr/ppermute | solution.py:13
  20.1 2.7 %copy.44 = f32[1,6,8192]{1,2,0:T(8,128)} copy(f32[1,6,8192]{2,0,1:T(1,128)S(1)} %collective-permute-done) | data formatting | bytes 393216 | tf_op jit(solution)/shard_map/while/body/eval_jaxpr/ppermute | solution.py:13
  22.8 5.0 %gather_fusion = f32[1024,6]{1,0:T(8,128)S(1)} fusion(f32[6,8192]{0,1:T(8,128)} %bitcast.114, s32[1024]{0:T(1024)S(1)} %broadcast_clamp_fusion.4), kind=kCustom, calls=%fused_computation.1.clone.clone.1 | custom fusion | bytes 53248 | tf_op jit(solution)/shard_map/while/body/eval_jaxpr/gather | solution.py:46
  33.6 5.0 %gather_fusion.1 = f32[1024,3]{1,0:T(8,128)S(1)} fusion(f32[3,8192]{0,1:T(8,128)} %get-tuple-element.399, s32[1024]{0:T(1024)S(1)} %broadcast_clamp_fusion.5), kind=kCustom, calls=%fused_computation.clone.clone.1 | custom fusion | bytes 28672 | tf_op jit(solution)/shard_map/while/body/eval_jaxpr/gather | solution.py:44
  38.6 3.5 %collective-permute-done = f32[1,6,8192]{2,0,1:T(1,128)S(1)} collective-permute-done((f32[1,6,8192]{2,0,1:T(1,128)S(1)}, f32[1,6,8192]{2,0,1:T(1,128)S(1)}, u32[]{:S(2)}, u32[]{:S(2)}) %collective-permute-start) | collective-permute-done | bytes 196640 | tf_op jit(solution)/shard_map/while/body/eval_jaxpr/ppermute | solution.py:13
  42.0 2.7 %copy.44 = f32[1,6,8192]{1,2,0:T(8,128)} copy(f32[1,6,8192]{2,0,1:T(1,128)S(1)} %collective-permute-done) | data formatting | bytes 393216 | tf_op jit(solution)/shard_map/while/body/eval_jaxpr/ppermute | solution.py:13
  44.7 5.0 %gather_fusion = f32[1024,6]{1,0:T(8,128)S(1)} fusion(f32[6,8192]{0,1:T(8,128)} %bitcast.114, s32[1024]{0:T(1024)S(1)} %broadcast_clamp_fusion.4), kind=kCustom, calls=%fused_computation.1.clone.clone.1 | custom fusion | bytes 53248 | tf_op jit(solution)/shard_map/while/body/eval_jaxpr/gather | solution.py:46
  55.5 5.0 %gather_fusion.1 = f32[1024,3]{1,0:T(8,128)S(1)} fusion(f32[3,8192]{0,1:T(8,128)} %get-tuple-element.399, s32[1024]{0:T(1024)S(1)} %broadcast_clamp_fusion.5), kind=kCustom, calls=%fused_computation.clone.clone.1 | custom fusion | bytes 28672 | tf_op jit(solution)/shard_map/while/body/eval_jaxpr/gather | solution.py:44
  60.5 2.8 %collective-permute-done = f32[1,6,8192]{2,0,1:T(1,128)S(1)} collective-permute-done((f32[1,6,8192]{2,0,1:T(1,128)S(1)}, f32[1,6,8192]{2,0,1:T(1,128)S(1)}, u32[]{:S(2)}, u32[]{:S(2)}) %collective-permute-start) | collective-permute-done | bytes 196640 | tf_op jit(solution)/shard_map/while/body/eval_jaxpr/ppermute | solution.py:13
  63.3 2.7 %copy.44 = f32[1,6,8192]{1,2,0:T(8,128)} copy(f32[1,6,8192]{2,0,1:T(1,128)S(1)} %collective-permute-done) | data formatting | bytes 393216 | tf_op jit(solution)/shard_map/while/body/eval_jaxpr/ppermute | solution.py:13
  66.0 5.0 %gather_fusion = f32[1024,6]{1,0:T(8,128)S(1)} fusion(f32[6,8192]{0,1:T(8,128)} %bitcast.114, s32[1024]{0:T(1024)S(1)} %broadcast_clamp_fusion.4), kind=kCustom, calls=%fused_computation.1.clone.clone.1 | custom fusion | bytes 53248 | tf_op jit(solution)/shard_map/while/body/eval_jaxpr/gather | solution.py:46
  76.8 5.0 %gather_fusion.1 = f32[1024,3]{1,0:T(8,128)S(1)} fusion(f32[3,8192]{0,1:T(8,128)} %get-tuple-element.399, s32[1024]{0:T(1024)S(1)} %broadcast_clamp_fusion.5), kind=kCustom, calls=%fused_computation.clone.clone.1 | custom fusion | bytes 28672 | tf_op jit(solution)/shard_map/while/body/eval_jaxpr/gather | solution.py:44
  81.8 2.8 %collective-permute-done = f32[1,6,8192]{2,0,1:T(1,128)S(1)} collective-permute-done((f32[1,6,8192]{2,0,1:T(1,128)S(1)}, f32[1,6,8192]{2,0,1:T(1,128)S(1)}, u32[]{:S(2)}, u32[]{:S(2)}) %collective-permute-start) | collective-permute-done | bytes 196640 | tf_op jit(solution)/shard_map/while/body/eval_jaxpr/ppermute | solution.py:13
  84.6 2.7 %copy.44 = f32[1,6,8192]{1,2,0:T(8,128)} copy(f32[1,6,8192]{2,0,1:T(1,128)S(1)} %collective-permute-done) | data formatting | bytes 393216 | tf_op jit(solution)/shard_map/while/body/eval_jaxpr/ppermute | solution.py:13
  87.3 5.0 %gather_fusion = f32[1024,6]{1,0:T(8,128)S(1)} fusion(f32[6,8192]{0,1:T(8,128)} %bitcast.114, s32[1024]{0:T(1024)S(1)} %broadcast_clamp_fusion.4), kind=kCustom, calls=%fused_computation.1.clone.clone.1 | custom fusion | bytes 53248 | tf_op jit(solution)/shard_map/while/body/eval_jaxpr/gather | solution.py:46
  98.1 5.0 %gather_fusion.1 = f32[1024,3]{1,0:T(8,128)S(1)} fusion(f32[3,8192]{0,1:T(8,128)} %get-tuple-element.399, s32[1024]{0:T(1024)S(1)} %broadcast_clamp_fusion.5), kind=kCustom, calls=%fused_computation.clone.clone.1 | custom fusion | bytes 28672 | tf_op jit(solution)/shard_map/while/body/eval_jaxpr/gather | solution.py:44
  103.1 2.8 %collective-permute-done = f32[1,6,8192]{2,0,1:T(1,128)S(1)} collective-permute-done((f32[1,6,8192]{2,0,1:T(1,128)S(1)}, f32[1,6,8192]{2,0,1:T(1,128)S(1)}, u32[]{:S(2)}, u32[]{:S(2)}) %collective-permute-start) | collective-permute-done | bytes 196640 | tf_op jit(solution)/shard_map/while/body/eval_jaxpr/ppermute | solution.py:13
  108.6 5.0 %gather_fusion = f32[1024,6]{1,0:T(8,128)S(1)} fusion(f32[6,8192]{0,1:T(8,128)} %bitcast.114, s32[1024]{0:T(1024)S(1)} %broadcast_clamp_fusion.4), kind=kCustom, calls=%fused_computation.1.clone.clone.1 | custom fusion | bytes 53248 | tf_op jit(solution)/shard_map/while/body/eval_jaxpr/gather | solution.py:46
  119.4 5.0 %gather_fusion.1 = f32[1024,3]{1,0:T(8,128)S(1)} fusion(f32[3,8192]{0,1:T(8,128)} %get-tuple-element.399, s32[1024]{0:T(1024)S(1)} %broadcast_clamp_fusion.5), kind=kCustom, calls=%fused_computation.clone.clone.1 | custom fusion | bytes 28672 | tf_op jit(solution)/shard_map/while/body/eval_jaxpr/gather | solution.py:44
  124.4 2.8 %collective-permute-done = f32[1,6,8192]{2,0,1:T(1,128)S(1)} collective-permute-done((f32[1,6,8192]{2,0,1:T(1,128)S(1)}, f32[1,6,8192]{2,0,1:T(1,128)S(1)}, u32[]{:S(2)}, u32[]{:S(2)}) %collective-permute-start) | collective-permute-done | bytes 196640 | tf_op jit(solution)/shard_map/while/body/eval_jaxpr/ppermute | solution.py:13
  129.9 5.0 %gather_fusion = f32[1024,6]{1,0:T(8,128)S(1)} fusion(f32[6,8192]{0,1:T(8,128)} %bitcast.114, s32[1024]{0:T(1024)S(1)} %broadcast_clamp_fusion.4), kind=kCustom, calls=%fused_computation.1.clone.clone.1 | custom fusion | bytes 53248 | tf_op jit(solution)/shard_map/while/body/eval_jaxpr/gather | solution.py:46
  140.7 5.0 %gather_fusion.1 = f32[1024,3]{1,0:T(8,128)S(1)} fusion(f32[3,8192]{0,1:T(8,128)} %get-tuple-element.399, s32[1024]{0:T(1024)S(1)} %broadcast_clamp_fusion.5), kind=kCustom, calls=%fused_computation.clone.clone.1 | custom fusion | bytes 28672 | tf_op jit(solution)/shard_map/while/body/eval_jaxpr/gather | solution.py:44
  145.7 2.8 %collective-permute-done = f32[1,6,8192]{2,0,1:T(1,128)S(1)} collective-permute-done((f32[1,6,8192]{2,0,1:T(1,128)S(1)}, f32[1,6,8192]{2,0,1:T(1,128)S(1)}, u32[]{:S(2)}, u32[]{:S(2)}) %collective-permute-start) | collective-permute-done | bytes 196640 | tf_op jit(solution)/shard_map/while/body/eval_jaxpr/ppermute | solution.py:13
  151.2 5.0 %gather_fusion = f32[1024,6]{1,0:T(8,128)S(1)} fusion(f32[6,8192]{0,1:T(8,128)} %bitcast.114, s32[1024]{0:T(1024)S(1)} %broadcast_clamp_fusion.4), kind=kCustom, calls=%fused_computation.1.clone.clone.1 | custom fusion | bytes 53248 | tf_op jit(solution)/shard_map/while/body/eval_jaxpr/gather | solution.py:46
  162.0 5.0 %gather_fusion.1 = f32[1024,3]{1,0:T(8,128)S(1)} fusion(f32[3,8192]{0,1:T(8,128)} %get-tuple-element.399, s32[1024]{0:T(1024)S(1)} %broadcast_clamp_fusion.5), kind=kCustom, calls=%fused_computation.clone.clone.1 | custom fusion | bytes 28672 | tf_op jit(solution)/shard_map/while/body/eval_jaxpr/gather | solution.py:44
  167.0 2.8 %collective-permute-done = f32[1,6,8192]{2,0,1:T(1,128)S(1)} collective-permute-done((f32[1,6,8192]{2,0,1:T(1,128)S(1)}, f32[1,6,8192]{2,0,1:T(1,128)S(1)}, u32[]{:S(2)}, u32[]{:S(2)}) %collective-permute-start) | collective-permute-done | bytes 196640 | tf_op jit(solution)/shard_map/while/body/eval_jaxpr/ppermute | solution.py:13
  172.5 5.0 %gather_fusion = f32[1024,6]{1,0:T(8,128)S(1)} fusion(f32[6,8192]{0,1:T(8,128)} %bitcast.114, s32[1024]{0:T(1024)S(1)} %broadcast_clamp_fusion.4), kind=kCustom, calls=%fused_computation.1.clone.clone.1 | custom fusion | bytes 53248 | tf_op jit(solution)/shard_map/while/body/eval_jaxpr/gather | solution.py:46
  182.1 9.5 %all-gather.1 = f32[16,1,1,36]{3,2,1,0:T(1,128)S(1)} all-gather(f32[8,1,1,36]{3,2,1,0:T(1,128)S(1)} %get-tuple-element.208), channel_id=3, replica_groups=mesh['blk'=128,'rep'=2] {'rep'}, dimensions={0}, use_global_device_ids=true | all-gather | bytes 3456 | tf_op jit(solution)/shard_map/all_gather | solution.py:17
  192.3 4.4 %all-gather.2 = f32[2,1,42]{2,1,0:T(1,128)S(1)} all-gather(f32[1,1,42]{2,1,0:T(1,128)S(1)} %fusion.24), channel_id=2, replica_groups=mesh['blk'=128,'rep'=2] {'rep'}, dimensions={0}, use_global_device_ids=true | all-gather | bytes 504 | tf_op jit(solution)/shard_map/all_gather | solution.py:17
  (262 shorter events, 62.9 us)
Async XLA Ops:
  0.6 3.5 %copy-start = (f32[1,3,8192]{2,0,1:T(1,128)S(1)}, f32[1,3,8192]{2,0,1:T(1,128)}, u32[]{:S(2)}) copy-start(f32[1,3,8192]{2,0,1:T(1,128)} %param.7) | copy-start | bytes 294916
  0.6 3.5 %copy-start.1 = (f32[1,3,8192]{2,0,1:T(1,128)S(1)}, f32[1,3,8192]{2,0,1:T(1,128)}, u32[]{:S(2)}) copy-start(f32[1,3,8192]{2,0,1:T(1,128)} %param.8) | copy-start | bytes 294916
  0.7 3.7 %copy-start.2 = (s32[8,1,1]{0,2,1:T(1,128)S(1)}, s32[8,1,1]{0,2,1:T(1,128)}, u32[]{:S(2)}) copy-start(s32[8,1,1]{0,2,1:T(1,128)} %param.11) | copy-start | bytes 100
  4.3 15.7 %collective-permute-start = (f32[1,6,8192]{2,0,1:T(1,128)S(1)}, f32[1,6,8192]{2,0,1:T(1,128)S(1)}, u32[]{:S(2)}, u32[]{:S(2)}) collective-permute-start(f32[1,6,8192]{2,0,1:T(1,128)S(1)} %get-tuple-element.380), channel_id=1, source_target_pairs={{254,0},{0,2},{2,4},{4,6},{6,8},{8,10},{10,12},{12,14},{14,16},{16... | collective-permute-start | bytes 589832 | tf_op jit(solution)/shard_map/while/body/eval_jaxpr/ppermute | solution.py:13
  6.5 24.7 %collective-permute-start.1 = (f32[1,42]{1,0:T(1,128)S(1)}, f32[1,42]{1,0:T(1,128)S(1)}, u32[]{:S(2)}, u32[]{:S(2)}) collective-permute-start(f32[1,42]{1,0:T(1,128)S(1)} %broadcast_select_fusion.4), channel_id=1, source_target_pairs={{254,0},{0,2},{2,4},{4,6},{6,8},{8,10},{10,12},{12,14},{14,16},{16... | collective-permute-start | bytes 512 | tf_op jit(solution)/shard_map/while/body/eval_jaxpr/ppermute | solution.py:13
  31.4 10.7 %collective-permute-start = (f32[1,6,8192]{2,0,1:T(1,128)S(1)}, f32[1,6,8192]{2,0,1:T(1,128)S(1)}, u32[]{:S(2)}, u32[]{:S(2)}) collective-permute-start(f32[1,6,8192]{2,0,1:T(1,128)S(1)} %get-tuple-element.380), channel_id=1, source_target_pairs={{254,0},{0,2},{2,4},{4,6},{6,8},{8,10},{10,12},{12,14},{14,16},{16... | collective-permute-start | bytes 589832 | tf_op jit(solution)/shard_map/while/body/eval_jaxpr/ppermute | solution.py:13
  31.4 21.8 %collective-permute-start.1 = (f32[1,42]{1,0:T(1,128)S(1)}, f32[1,42]{1,0:T(1,128)S(1)}, u32[]{:S(2)}, u32[]{:S(2)}) collective-permute-start(f32[1,42]{1,0:T(1,128)S(1)} %broadcast_select_fusion.4), channel_id=1, source_target_pairs={{254,0},{0,2},{2,4},{4,6},{6,8},{8,10},{10,12},{12,14},{14,16},{16... | collective-permute-start | bytes 512 | tf_op jit(solution)/shard_map/while/body/eval_jaxpr/ppermute | solution.py:13
  53.3 10.0 %collective-permute-start = (f32[1,6,8192]{2,0,1:T(1,128)S(1)}, f32[1,6,8192]{2,0,1:T(1,128)S(1)}, u32[]{:S(2)}, u32[]{:S(2)}) collective-permute-start(f32[1,6,8192]{2,0,1:T(1,128)S(1)} %get-tuple-element.380), channel_id=1, source_target_pairs={{254,0},{0,2},{2,4},{4,6},{6,8},{8,10},{10,12},{12,14},{14,16},{16... | collective-permute-start | bytes 589832 | tf_op jit(solution)/shard_map/while/body/eval_jaxpr/ppermute | solution.py:13
  53.4 21.1 %collective-permute-start.1 = (f32[1,42]{1,0:T(1,128)S(1)}, f32[1,42]{1,0:T(1,128)S(1)}, u32[]{:S(2)}, u32[]{:S(2)}) collective-permute-start(f32[1,42]{1,0:T(1,128)S(1)} %broadcast_select_fusion.4), channel_id=1, source_target_pairs={{254,0},{0,2},{2,4},{4,6},{6,8},{8,10},{10,12},{12,14},{14,16},{16... | collective-permute-start | bytes 512 | tf_op jit(solution)/shard_map/while/body/eval_jaxpr/ppermute | solution.py:13
  74.6 10.0 %collective-permute-start = (f32[1,6,8192]{2,0,1:T(1,128)S(1)}, f32[1,6,8192]{2,0,1:T(1,128)S(1)}, u32[]{:S(2)}, u32[]{:S(2)}) collective-permute-start(f32[1,6,8192]{2,0,1:T(1,128)S(1)} %get-tuple-element.380), channel_id=1, source_target_pairs={{254,0},{0,2},{2,4},{4,6},{6,8},{8,10},{10,12},{12,14},{14,16},{16... | collective-permute-start | bytes 589832 | tf_op jit(solution)/shard_map/while/body/eval_jaxpr/ppermute | solution.py:13
  74.7 21.1 %collective-permute-start.1 = (f32[1,42]{1,0:T(1,128)S(1)}, f32[1,42]{1,0:T(1,128)S(1)}, u32[]{:S(2)}, u32[]{:S(2)}) collective-permute-start(f32[1,42]{1,0:T(1,128)S(1)} %broadcast_select_fusion.4), channel_id=1, source_target_pairs={{254,0},{0,2},{2,4},{4,6},{6,8},{8,10},{10,12},{12,14},{14,16},{16... | collective-permute-start | bytes 512 | tf_op jit(solution)/shard_map/while/body/eval_jaxpr/ppermute | solution.py:13
  95.9 10.0 %collective-permute-start = (f32[1,6,8192]{2,0,1:T(1,128)S(1)}, f32[1,6,8192]{2,0,1:T(1,128)S(1)}, u32[]{:S(2)}, u32[]{:S(2)}) collective-permute-start(f32[1,6,8192]{2,0,1:T(1,128)S(1)} %get-tuple-element.380), channel_id=1, source_target_pairs={{254,0},{0,2},{2,4},{4,6},{6,8},{8,10},{10,12},{12,14},{14,16},{16... | collective-permute-start | bytes 589832 | tf_op jit(solution)/shard_map/while/body/eval_jaxpr/ppermute | solution.py:13
  96.0 21.1 %collective-permute-start.1 = (f32[1,42]{1,0:T(1,128)S(1)}, f32[1,42]{1,0:T(1,128)S(1)}, u32[]{:S(2)}, u32[]{:S(2)}) collective-permute-start(f32[1,42]{1,0:T(1,128)S(1)} %broadcast_select_fusion.4), channel_id=1, source_target_pairs={{254,0},{0,2},{2,4},{4,6},{6,8},{8,10},{10,12},{12,14},{14,16},{16... | collective-permute-start | bytes 512 | tf_op jit(solution)/shard_map/while/body/eval_jaxpr/ppermute | solution.py:13
  117.2 10.0 %collective-permute-start = (f32[1,6,8192]{2,0,1:T(1,128)S(1)}, f32[1,6,8192]{2,0,1:T(1,128)S(1)}, u32[]{:S(2)}, u32[]{:S(2)}) collective-permute-start(f32[1,6,8192]{2,0,1:T(1,128)S(1)} %get-tuple-element.380), channel_id=1, source_target_pairs={{254,0},{0,2},{2,4},{4,6},{6,8},{8,10},{10,12},{12,14},{14,16},{16... | collective-permute-start | bytes 589832 | tf_op jit(solution)/shard_map/while/body/eval_jaxpr/ppermute | solution.py:13
  117.3 21.1 %collective-permute-start.1 = (f32[1,42]{1,0:T(1,128)S(1)}, f32[1,42]{1,0:T(1,128)S(1)}, u32[]{:S(2)}, u32[]{:S(2)}) collective-permute-start(f32[1,42]{1,0:T(1,128)S(1)} %broadcast_select_fusion.4), channel_id=1, source_target_pairs={{254,0},{0,2},{2,4},{4,6},{6,8},{8,10},{10,12},{12,14},{14,16},{16... | collective-permute-start | bytes 512 | tf_op jit(solution)/shard_map/while/body/eval_jaxpr/ppermute | solution.py:13
  138.5 10.0 %collective-permute-start = (f32[1,6,8192]{2,0,1:T(1,128)S(1)}, f32[1,6,8192]{2,0,1:T(1,128)S(1)}, u32[]{:S(2)}, u32[]{:S(2)}) collective-permute-start(f32[1,6,8192]{2,0,1:T(1,128)S(1)} %get-tuple-element.380), channel_id=1, source_target_pairs={{254,0},{0,2},{2,4},{4,6},{6,8},{8,10},{10,12},{12,14},{14,16},{16... | collective-permute-start | bytes 589832 | tf_op jit(solution)/shard_map/while/body/eval_jaxpr/ppermute | solution.py:13
  138.5 21.1 %collective-permute-start.1 = (f32[1,42]{1,0:T(1,128)S(1)}, f32[1,42]{1,0:T(1,128)S(1)}, u32[]{:S(2)}, u32[]{:S(2)}) collective-permute-start(f32[1,42]{1,0:T(1,128)S(1)} %broadcast_select_fusion.4), channel_id=1, source_target_pairs={{254,0},{0,2},{2,4},{4,6},{6,8},{8,10},{10,12},{12,14},{14,16},{16... | collective-permute-start | bytes 512 | tf_op jit(solution)/shard_map/while/body/eval_jaxpr/ppermute | solution.py:13
  159.8 10.0 %collective-permute-start = (f32[1,6,8192]{2,0,1:T(1,128)S(1)}, f32[1,6,8192]{2,0,1:T(1,128)S(1)}, u32[]{:S(2)}, u32[]{:S(2)}) collective-permute-start(f32[1,6,8192]{2,0,1:T(1,128)S(1)} %get-tuple-element.380), channel_id=1, source_target_pairs={{254,0},{0,2},{2,4},{4,6},{6,8},{8,10},{10,12},{12,14},{14,16},{16... | collective-permute-start | bytes 589832 | tf_op jit(solution)/shard_map/while/body/eval_jaxpr/ppermute | solution.py:13
  159.8 21.1 %collective-permute-start.1 = (f32[1,42]{1,0:T(1,128)S(1)}, f32[1,42]{1,0:T(1,128)S(1)}, u32[]{:S(2)}, u32[]{:S(2)}) collective-permute-start(f32[1,42]{1,0:T(1,128)S(1)} %broadcast_select_fusion.4), channel_id=1, source_target_pairs={{254,0},{0,2},{2,4},{4,6},{6,8},{8,10},{10,12},{12,14},{14,16},{16... | collective-permute-start | bytes 512 | tf_op jit(solution)/shard_map/while/body/eval_jaxpr/ppermute | solution.py:13
  181.1 11.1 %collective-permute-start.2 = (f32[1,42]{1,0:T(1,128)S(1)}, f32[1,42]{1,0:T(1,128)S(1)}, u32[]{:S(2)}, u32[]{:S(2)}) collective-permute-start(f32[1,42]{1,0:T(1,128)S(1)} %get-tuple-element.207), channel_id=1, source_target_pairs={{16,0},{18,2},{20,4},{22,6},{24,8},{26,10},{28,12},{30,14},{32,16}... | collective-permute-start | bytes 512 | tf_op jit(solution)/shard_map/ppermute | solution.py:13
where the time goes:
time: 199 us; the launch traced here: 198 us
  local copies, waits for them, and re-layouts  122 us (61%)
  other arithmetic  26.9 us (14%)
  waiting for transfers between devices  25.3 us (13%)
  blocking collectives  14 us (7%)
  starting transfers between devices  5.33 us (3%)
  matrix products  2.67 us (1%)
    gather x8, local copies, waits for them, and re-layouts, round_terms(): picked = flat_tgt[:, tidx]  39.9 us
    gather x8, local copies, waits for them, and re-layouts, round_terms(): p = flat_src[:, sidx]  39.9 us
    ppermute x17, waiting for transfers between devices, passed_along(): return lax.ppermute(block, axis, route)  25.3 us
    ppermute x8, local copies, waits for them, and re-layouts, passed_along(): return lax.ppermute(block, axis, route)  21.6 us
    all_gather x2, blocking collectives, total_of_pieces(): pieces = lax.all_gather(shard, axis)  14 us
    sub x8, other arithmetic, round_terms(): p[1] * n[2] - p[2] * n[1]  9.92 us
    dynamic_slice x8, local copies, waits for them, and re-layouts, round_terms(): lax.dynamic_index_in_dim(tgt_index, k, 0, keepdims=False)  5.54 us
    ppermute x17, starting transfers between devices, passed_along(): return lax.ppermute(block, axis, route)  5.33 us
  transfers between devices with their start and end apart: 17, of which 8 were waited for; matrix products, arithmetic and copies ran while one was open for 74% of the time, Pallas kernels for 0%

commit v1 on v0

v1 whole, which is shorter than its diff:
```python
import functools

import jax
import jax.numpy as jnp
from jax import lax
from jax.experimental import pallas as pl
from jax.experimental.pallas import tpu as pltpu
from jax.sharding import PartitionSpec as P

MESH = pl.DeviceIdType.MESH
LANES = 128
ENTRIES = [(i, j) for i in range(6) for j in range(i, 6)]


def kernel(
    n_blk, rounds, nslots, npts, total_slots,
    pts_hbm, nrm_hbm, src_hbm, tgt_hbm, act_hbm,
    diag_ref, grad_ref, pair_ref,
    pts, nrm, tgt, src, act,
    p_send, a_send, i_recv, p_recv, a_recv,
    prods, r_send, r_recv, t_send, t_recv,
    local_sem, i_ssem, i_rsem, p_ssem, p_rsem, a_ssem, a_rsem,
    r_ssem, r_rsem, t_ssem, t_rsem,
):
    me = lax.axis_index("blk")
    rep = lax.axis_index("rep")
    rows = npts // LANES

    def up(k):
        return lax.rem(me + k, n_blk)

    def down(k):
        return lax.rem(me + n_blk - k, n_blk)

    barrier = pltpu.get_barrier_semaphore()
    for k in range(1, rounds + 1):
        pl.semaphore_signal(barrier, inc=1, device_id=(up(k), rep), device_id_type=MESH)
        for half in range(2):
            pl.semaphore_signal(barrier, inc=1, device_id=(down(k), half), device_id_type=MESH)
    pl.semaphore_signal(barrier, inc=1, device_id=(me, 1 - rep), device_id_type=MESH)

    loads = [
        pltpu.make_async_copy(src_hbm, src, local_sem.at[0]),
        pltpu.make_async_copy(act_hbm, act, local_sem.at[1]),
        pltpu.make_async_copy(pts_hbm, pts, local_sem.at[2]),
        pltpu.make_async_copy(tgt_hbm, tgt, local_sem.at[3]),
        pltpu.make_async_copy(nrm_hbm, nrm, local_sem.at[4]),
    ]
    for load in loads:
        load.start()
    for load in loads:
        load.wait()

    for k in range(rounds):
        for j in range(nslots):
            block = src[k, j]
            for c in range(3):
                p_send[k, c, pl.ds(j, 1), :] = pts[c, pl.ds(block, 1), :]
        a_send[k] = jnp.full((1, LANES), act[0, k], jnp.int32)

    pl.semaphore_wait(barrier, 3 * rounds + 1)

    sends = []
    order = list(range(rounds))
    for k in reversed(order):
        to = (down(k + 1), rep)
        for source, target, ssem, rsem in (
            (tgt.at[k], i_recv.at[k], i_ssem.at[k], i_rsem.at[k]),
            (a_send.at[k], a_recv.at[k], a_ssem.at[k], a_rsem.at[k]),
            (p_send.at[k], p_recv.at[k], p_ssem.at[k], p_rsem.at[k]),
        ):
            copy = pltpu.make_async_remote_copy(
                src_ref=source, dst_ref=target, send_sem=ssem, recv_sem=rsem,
                device_id=to, device_id_type=MESH,
            )
            copy.start()
            sends.append((k, copy))

    sub = lax.broadcasted_iota(jnp.int32, (nslots, LANES), 0)
    lane = lax.broadcasted_iota(jnp.int32, (nslots, LANES), 1)
    slot_of = sub + rep * nslots
    li, lj = lane // 6, lane % 6
    lo, hi = jnp.minimum(li, lj), jnp.maximum(li, lj)
    entry_of = jnp.where(
        lane < 36, lo * 6 - (lo * (lo - 1)) // 2 + hi - lo,
        jnp.where(lane < 42, lane - 36 + 21, -1),
    )

    tsum = jnp.zeros((1, LANES), jnp.float32)
    results = []
    for k in order:
        inbound = [copy for kk, copy in sends if kk == k]
        inbound[0].wait_recv()
        index = i_recv[k]
        row_of = index // LANES
        lane_of = index % LANES

        def gather_rows(g, acc):
            acc = list(acc)
            base = pl.multiple_of(g * 8, 8)
            for table, first in ((pts, 0), (nrm, 3)):
                for c in range(3):
                    tile = table[c, pl.ds(base, 8), :]
                    for j in range(8):
                        row = jnp.broadcast_to(tile[j : j + 1], (nslots, LANES))
                        got = jnp.take_along_axis(row, lane_of, axis=1, mode="promise_in_bounds")
                        acc[first + c] = jnp.where(row_of == base + j, got, acc[first + c])
            return tuple(acc)

        zero = jnp.zeros((nslots, LANES), jnp.float32)
        q0, q1, q2, n0, n1, n2 = lax.fori_loop(0, rows // 8, gather_rows, (zero,) * 6)

        inbound[1].wait_recv()
        inbound[2].wait_recv()
        live = (slot_of < a_recv[k]).astype(jnp.float32)
        p0, p1, p2 = p_recv[k, 0], p_recv[k, 1], p_recv[k, 2]
        resid = n0 * (p0 - q0) + n1 * (p1 - q1) + n2 * (p2 - q2)
        weight = live / (1.0 + resid * resid)
        jacob = [p1 * n2 - p2 * n1, p2 * n0 - p0 * n2, p0 * n1 - p1 * n0, n0, n1, n2]
        scaled = [weight * entry for entry in jacob]
        for e, (i, j) in enumerate(ENTRIES):
            prods[pl.ds(e * 8, 8), :] = scaled[i] * jacob[j]
        for i in range(6):
            prods[pl.ds((21 + i) * 8, 8), :] = scaled[i] * resid
        spread = jnp.zeros((8, LANES), jnp.float32)
        for g in range(4):
            some = prods[pl.ds(g * 64, 8, stride=8), :]
            for t in range(1, 8):
                some = some + prods[pl.ds(g * 64 + t, 8, stride=8), :]
            whole = jnp.sum(some, axis=1, keepdims=True)
            spread = spread + jnp.where(entry_of == sub + g * 8, whole, 0.0)
        line = jnp.sum(spread, axis=0, keepdims=True)
        tsum = tsum + line
        r_send[k] = line
        for half in range(2):
            copy = pltpu.make_async_remote_copy(
                src_ref=r_send.at[k], dst_ref=r_recv.at[rep, k],
                send_sem=r_ssem.at[half, k], recv_sem=r_rsem.at[rep, k],
                device_id=(up(k + 1), half), device_id_type=MESH,
            )
            copy.start()
            results.append(copy)

    t_send[...] = tsum
    exchange = pltpu.make_async_remote_copy(
        src_ref=t_send, dst_ref=t_recv, send_sem=t_ssem, recv_sem=t_rsem,
        device_id=(me, 1 - rep), device_id_type=MESH,
    )
    exchange.start()

    lane1 = lax.broadcasted_iota(jnp.int32, (1, LANES), 1)
    source_sum = jnp.zeros((1, LANES), jnp.float32)
    for k in order:
        for half in range(2):
            pltpu.make_async_remote_copy(
                src_ref=r_send.at[k], dst_ref=r_recv.at[half, k],
                send_sem=r_ssem.at[half, k], recv_sem=r_rsem.at[half, k],
                device_id=(up(k + 1), half), device_id_type=MESH,
            ).wait_recv()
        both = (r_recv[0, k] + r_recv[1, k]) * (1.0 / total_slots)
        pair_ref[pl.ds(k, 1), :] = both[:, :36]
        source_sum = source_sum + both
    exchange.wait_recv()
    target_sum = (t_send[...] + t_recv[...]) * (1.0 / total_slots)
    final = (source_sum + jnp.where(lane1 < 36, target_sum, -target_sum)) * (1.0 / (2.0 * rounds))
    diag_ref[...] = final[:, :36]
    grad_ref[...] = final[:, 36:42]

    for _, copy in sends:
        copy.wait_send()
    for copy in results:
        copy.wait_send()
    exchange.wait_send()


def solution(mesh):
    n_blk = mesh.shape["blk"]

    def body(points, normals, src_block, tgt_index, active):
        npts = points.shape[2]
        rounds, nslots = src_block.shape[0], src_block.shape[3]
        rows = npts // LANES
        f32, i32 = jnp.float32, jnp.int32
        dma = pltpu.SemaphoreType.DMA
        diag, grad, pair = pl.pallas_call(
            functools.partial(kernel, n_blk, rounds, nslots, npts, 2 * nslots * LANES),
            out_shape=(
                jax.ShapeDtypeStruct((1, 36), f32),
                jax.ShapeDtypeStruct((1, 6), f32),
                jax.ShapeDtypeStruct((rounds, 36), f32),
            ),
            in_specs=[pl.BlockSpec(memory_space=pl.ANY)] * 5,
            out_specs=(pl.BlockSpec(memory_space=pltpu.VMEM),) * 3,
            scratch_shapes=[
                pltpu.VMEM((3, rows, LANES), f32),
                pltpu.VMEM((3, rows, LANES), f32),
                pltpu.VMEM((rounds, nslots, LANES), i32),
                pltpu.SMEM((rounds, nslots), i32),
                pltpu.SMEM((1, rounds), i32),
                pltpu.VMEM((rounds, 3, nslots, LANES), f32),
                pltpu.VMEM((rounds, 1, LANES), i32),
                pltpu.VMEM((rounds, nslots, LANES), i32),
                pltpu.VMEM((rounds, 3, nslots, LANES), f32),
                pltpu.VMEM((rounds, 1, LANES), i32),
                pltpu.VMEM((256, LANES), f32),
                pltpu.VMEM((rounds, 1, LANES), f32),
                pltpu.VMEM((2, rounds, 1, LANES), f32),
                pltpu.VMEM((1, LANES), f32),
                pltpu.VMEM((1, LANES), f32),
                dma((5,)),
                dma((rounds,)), dma((rounds,)),
                dma((rounds,)), dma((rounds,)),
                dma((rounds,)), dma((rounds,)),
                dma((2, rounds)), dma((2, rounds)),
                dma, dma,
            ],
            compiler_params=pltpu.CompilerParams(collective_id=0, has_side_effects=True),
        )(
            points.reshape(3, rows, LANES),
            normals.reshape(3, rows, LANES),
            src_block.reshape(rounds, nslots),
            tgt_index.reshape(rounds, nslots, LANES),
            active.reshape(1, rounds),
        )
        return diag, grad, pair.reshape(rounds, 1, 1, 36)

    return jax.shard_map(
        body,
        mesh=mesh,
        in_specs=(
            P("blk", None, None),
            P("blk", None, None),
            P(None, "blk", None, "rep"),
            P(None, "blk", None, "rep", None),
            P(None, "blk", None),
        ),
        out_specs=(P("blk", None), P("blk", None), P(None, "blk", None, None)),
        check_vma=False,
    )
```

time: 199 us -> 34 us (0.17)
  the two profiles are of different devices: /device:TPU:1 before, /device:TPU:26 now
where the time goes in v1:
time: 34 us; the launch traced here: 33.8 us
  Pallas kernels  30.8 us (91%)
  local copies, waits for them, and re-layouts  2.29 us (7%)
  between operations  0.66 us (2%)
    pallas_call x1, Pallas kernels, body(): pl.pallas_call(functools.partial(kernel, n_blk, rounds, nslots, npts, 2 *...  30.8 us
    unnamed x9, local copies, waits for them, and re-layouts  2.29 us

profile of v1, /device:TPU:26, one launch (start us, length us, event | category | flops | bytes accessed | tf_op | source)
XLA Modules:
  0.0 33.8 jit_solution(6111690597808088600)
XLA Ops:
  0.6 30.8 %shard_map.76 = (f32[1,36]{1,0:T(1,128)}, f32[1,6]{1,0:T(1,128)}, f32[8,36]{1,0:T(8,128)}) custom-call(f32[3,64,128]{2,1,0:T(8,128)} %bitcast.8, f32[3,64,128]{2,1,0:T(8,128)} %bitcast.9, s32[8,8]{1,0:T(8,128)} %bitcast.11, s32[8,8,128]{2,1,0:T(8,128)} %bitcast.10, s32[1,8]{1,0:T(1,128)} %bitcast.13), custom_call_target="tpu_custom_call" | custom-call | tf_op jit(solution)/shard_map/pallas_call | solution.py:185
  31.5 0.0 copy-start.2
  31.5 0.0 copy-start
  31.5 0.6 %copy-done.2 = f32[1,36]{1,0:T(1,128)S(1)} copy-done((f32[1,36]{1,0:T(1,128)S(1)}, f32[1,36]{1,0:T(1,128)}, u32[]{:S(2)}) %copy-start.2) | copy-done | bytes 168
  32.1 0.0 copy-start.1
  32.1 0.5 %copy.12 = f32[1,36]{1,0:T(1,128)} copy(f32[1,36]{1,0:T(1,128)S(1)} %copy-done.2) | data formatting | bytes 288
  32.6 0.1 copy-done.1
  32.7 0.5 %copy.13 = f32[1,6]{1,0:T(1,128)} copy(f32[1,6]{1,0:T(1,128)S(1)} %copy-done.1) | data formatting | bytes 48
  33.2 0.0 copy-done
  33.2 0.6 %copy.14 = f32[8,1,1,36]{3,2,1,0:T(1,128)} copy(f32[8,1,1,36]{3,2,1,0:T(1,128)S(1)} %bitcast.12) | data formatting | bytes 2304
Async XLA Ops:
  31.5 0.6 %copy-start.2 = (f32[1,36]{1,0:T(1,128)S(1)}, f32[1,36]{1,0:T(1,128)}, u32[]{:S(2)}) copy-start(f32[1,36]{1,0:T(1,128)} %get-tuple-element.15) | copy-start | bytes 436
  31.5 1.7 %copy-start = (f32[8,36]{1,0:T(8,128)S(1)}, f32[8,36]{1,0:T(8,128)}, u32[]{:S(2)}) copy-start(f32[8,36]{1,0:T(8,128)} %get-tuple-element.8) | copy-start | bytes 3460
  32.1 0.6 %copy-start.1 = (f32[1,6]{1,0:T(1,128)S(1)}, f32[1,6]{1,0:T(1,128)}, u32[]{:S(2)}) copy-start(f32[1,6]{1,0:T(1,128)} %get-tuple-element.16) | copy-start | bytes 76

commit v2 on v1

--- a/solution.py
+++ b/solution.py
@@ -13,9 +13,9 @@
 
 
 def kernel(
-    n_blk, rounds, nslots, npts, total_slots,
+    n_blk, rounds, nslots, npts,
     pts_hbm, nrm_hbm, src_hbm, tgt_hbm, act_hbm,
-    diag_ref, grad_ref, pair_ref,
+    out_ref,
     pts, nrm, tgt, src, act,
     p_send, a_send, i_recv, p_recv, a_recv,
     prods, r_send, r_recv, t_send, t_recv,
@@ -86,32 +86,36 @@
         jnp.where(lane < 42, lane - 36 + 21, -1),
     )
 
-    tsum = jnp.zeros((1, LANES), jnp.float32)
-    results = []
-    for k in order:
-        inbound = [copy for kk, copy in sends if kk == k]
-        inbound[0].wait_recv()
+    def inbound(k, source, target, ssem, rsem):
+        return pltpu.make_async_remote_copy(
+            src_ref=source.at[k], dst_ref=target.at[k], send_sem=ssem.at[k], recv_sem=rsem.at[k],
+            device_id=(down(k + 1), rep), device_id_type=MESH,
+        )
+
+    def returned(k, half):
+        return pltpu.make_async_remote_copy(
+            src_ref=r_send.at[k], dst_ref=r_recv.at[rep, k],
+            send_sem=r_ssem.at[half, k], recv_sem=r_rsem.at[rep, k],
+            device_id=(up(k + 1), half), device_id_type=MESH,
+        )
+
+    def one_pair(step, tsum):
+        k = rounds - 1 - step
+        inbound(k, tgt, i_recv, i_ssem, i_rsem).wait_recv()
         index = i_recv[k]
-        row_of = index // LANES
-        lane_of = index % LANES
-
-        def gather_rows(g, acc):
-            acc = list(acc)
-            base = pl.multiple_of(g * 8, 8)
-            for table, first in ((pts, 0), (nrm, 3)):
-                for c in range(3):
-                    tile = table[c, pl.ds(base, 8), :]
-                    for j in range(8):
-                        row = jnp.broadcast_to(tile[j : j + 1], (nslots, LANES))
-                        got = jnp.take_along_axis(row, lane_of, axis=1, mode="promise_in_bounds")
-                        acc[first + c] = jnp.where(row_of == base + j, got, acc[first + c])
-            return tuple(acc)
-
-        zero = jnp.zeros((nslots, LANES), jnp.float32)
-        q0, q1, q2, n0, n1, n2 = lax.fori_loop(0, rows // 8, gather_rows, (zero,) * 6)
-
-        inbound[1].wait_recv()
-        inbound[2].wait_recv()
+        row_of = lax.shift_right_logical(index, 7)
+        lane_of = lax.bitwise_and(index, LANES - 1)
+        acc = [jnp.zeros((nslots, LANES), jnp.float32)] * 6
+        for row in range(rows):
+            here = row_of == row
+            for e, (table, c) in enumerate(((pts, 0), (pts, 1), (pts, 2), (nrm, 0), (nrm, 1), (nrm, 2))):
+                line = jnp.broadcast_to(table[c, row : row + 1, :], (nslots, LANES))
+                got = jnp.take_along_axis(line, lane_of, axis=1, mode="promise_in_bounds")
+                acc[e] = jnp.where(here, got, acc[e])
+        q0, q1, q2, n0, n1, n2 = acc
+
+        inbound(k, a_send, a_recv, a_ssem, a_rsem).wait_recv()
+        inbound(k, p_send, p_recv, p_ssem, p_rsem).wait_recv()
         live = (slot_of < a_recv[k]).astype(jnp.float32)
         p0, p1, p2 = p_recv[k, 0], p_recv[k, 1], p_recv[k, 2]
         resid = n0 * (p0 - q0) + n1 * (p1 - q1) + n2 * (p2 - q2)
@@ -130,17 +134,12 @@
             whole = jnp.sum(some, axis=1, keepdims=True)
             spread = spread + jnp.where(entry_of == sub + g * 8, whole, 0.0)
         line = jnp.sum(spread, axis=0, keepdims=True)
-        tsum = tsum + line
         r_send[k] = line
         for half in range(2):
-            copy = pltpu.make_async_remote_copy(
-                src_ref=r_send.at[k], dst_ref=r_recv.at[rep, k],
-                send_sem=r_ssem.at[half, k], recv_sem=r_rsem.at[rep, k],
-                device_id=(up(k + 1), half), device_id_type=MESH,
-            )
-            copy.start()
-            results.append(copy)
-
+            returned(k, half).start()
+        return tsum + line
+
+    tsum = lax.fori_loop(0, rounds, one_pair, jnp.zeros((1, LANES), jnp.float32))
     t_send[...] = tsum
     exchange = pltpu.make_async_remote_copy(
         src_ref=t_send, dst_ref=t_recv, send_sem=t_ssem, recv_sem=t_rsem,
@@ -148,29 +147,35 @@
     )
     exchange.start()
 
-    lane1 = lax.broadcasted_iota(jnp.int32, (1, LANES), 1)
     source_sum = jnp.zeros((1, LANES), jnp.float32)
-    for k in order:
+    for k in reversed(order):
         for half in range(2):
             pltpu.make_async_remote_copy(
                 src_ref=r_send.at[k], dst_ref=r_recv.at[half, k],
                 send_sem=r_ssem.at[half, k], recv_sem=r_rsem.at[half, k],
                 device_id=(up(k + 1), half), device_id_type=MESH,
             ).wait_recv()
-        both = (r_recv[0, k] + r_recv[1, k]) * (1.0 / total_slots)
-        pair_ref[pl.ds(k, 1), :] = both[:, :36]
+        both = r_recv[0, k] + r_recv[1, k]
+        out_ref[pl.ds(k, 1), :] = both
         source_sum = source_sum + both
     exchange.wait_recv()
-    target_sum = (t_send[...] + t_recv[...]) * (1.0 / total_slots)
-    final = (source_sum + jnp.where(lane1 < 36, target_sum, -target_sum)) * (1.0 / (2.0 * rounds))
-    diag_ref[...] = final[:, :36]
-    grad_ref[...] = final[:, 36:42]
+    target_sum = t_send[...] + t_recv[...]
+    lane1 = lax.broadcasted_iota(jnp.int32, (1, LANES), 1)
+    out_ref[pl.ds(rounds, 1), :] = source_sum + jnp.where(lane1 < 36, target_sum, -target_sum)
 
     for _, copy in sends:
         copy.wait_send()
-    for copy in results:
-        copy.wait_send()
+    for k in order:
+        for half in range(2):
+            returned(k, half).wait_send()
     exchange.wait_send()
+
+
+def finish(rounds, total_slots, sums_ref, diag_ref, grad_ref, pair_ref):
+    pair_ref[...] = sums_ref[:rounds, :36] * (1.0 / total_slots)
+    total = sums_ref[rounds : rounds + 1] * (1.0 / (total_slots * 2.0 * rounds))
+    diag_ref[...] = total[:, :36]
+    grad_ref[...] = total[:, 36:42]
 
 
 def solution(mesh):
@@ -182,15 +187,12 @@
         rows = npts // LANES
         f32, i32 = jnp.float32, jnp.int32
         dma = pltpu.SemaphoreType.DMA
-        diag, grad, pair = pl.pallas_call(
-            functools.partial(kernel, n_blk, rounds, nslots, npts, 2 * nslots * LANES),
-            out_shape=(
-                jax.ShapeDtypeStruct((1, 36), f32),
-                jax.ShapeDtypeStruct((1, 6), f32),
-                jax.ShapeDtypeStruct((rounds, 36), f32),
-            ),
+        total_slots = 2 * nslots * LANES
+        sums = pl.pallas_call(
+            functools.partial(kernel, n_blk, rounds, nslots, npts),
+            out_shape=jax.ShapeDtypeStruct((rounds + 8, LANES), f32),
             in_specs=[pl.BlockSpec(memory_space=pl.ANY)] * 5,
-            out_specs=(pl.BlockSpec(memory_space=pltpu.VMEM),) * 3,
+            out_specs=pl.BlockSpec(memory_space=pltpu.VMEM),
             scratch_shapes=[
                 pltpu.VMEM((3, rows, LANES), f32),
                 pltpu.VMEM((3, rows, LANES), f32),
@@ -214,14 +216,23 @@
                 dma((2, rounds)), dma((2, rounds)),
                 dma, dma,
             ],
-            compiler_params=pltpu.CompilerParams(collective_id=0, has_side_effects=True),
+            compiler_params=pltpu.CompilerParams(collective_id=0, has_side_effects=True, vmem_limit_bytes=8 * 1024 * 1024),
         )(
-            points.reshape(3, rows, LANES),
-            normals.reshape(3, rows, LANES),
-            src_block.reshape(rounds, nslots),
-            tgt_index.reshape(rounds, nslots, LANES),
-            active.reshape(1, rounds),
+            pltpu.with_memory_space_constraint(points.reshape(3, rows, LANES), pltpu.HBM),
+            pltpu.with_memory_space_constraint(normals.reshape(3, rows, LANES), pltpu.HBM),
+            pltpu.with_memory_space_constraint(src_block.reshape(rounds, nslots), pltpu.HBM),
+            pltpu.with_memory_space_constraint(tgt_index.reshape(rounds, nslots, LANES), pltpu.HBM),
+            pltpu.with_memory_space_constraint(active.reshape(1, rounds), pltpu.HBM),
         )
+        diag, grad, pair = pl.pallas_call(
+            functools.partial(finish, rounds, total_slots),
+            out_shape=(
+                jax.ShapeDtypeStruct((1, 36), f32),
+                jax.ShapeDtypeStruct((1, 6), f32),
+                jax.ShapeDtypeStruct((rounds, 36), f32),
+            ),
+            compiler_params=pltpu.CompilerParams(vmem_limit_bytes=1024 * 1024),
+        )(sums)
         return diag, grad, pair.reshape(rounds, 1, 1, 36)
 
     return jax.shard_map(

time: 34 us -> 29.4 us (0.86)
  the two profiles are of different devices: /device:TPU:26 before, /device:TPU:1 now
where the time goes in v2:
time: 29.4 us; the launch traced here: 29.3 us
  Pallas kernels  28.6 us (97%)
  between operations  0.64 us (2%)
    pallas_call x1, Pallas kernels, body(): pl.pallas_call(functools.partial(kernel, n_blk, rounds, nslots, npts), ou...  28 us
    pallas_call x1, Pallas kernels, body(): pl.pallas_call(functools.partial(finish, rounds, total_slots), out_shape=...  0.67 us

profile of v2, /device:TPU:1, one launch (start us, length us, event | category | flops | bytes accessed | tf_op | source)
XLA Modules:
  0.0 29.3 jit_solution(17806258012811730552)
XLA Ops:
  0.6 28.0 %shard_map.76.sums_ref = f32[16,128]{1,0:T(8,128)S(1)} custom-call(f32[3,64,128]{2,1,0:T(8,128)} %bitcast.8, f32[3,64,128]{2,1,0:T(8,128)} %bitcast.9, s32[8,8]{1,0:T(8,128)} %bitcast.11, s32[8,8,128]{2,1,0:T(8,128)} %bitcast.10, s32[1,8]{1,0:T(1,128)} %bitcast.12), custom_call_target="tpu_custom_call" | custom-call | tf_op jit(solution)/shard_map/pallas_call | solution.py:191
  28.6 0.7 %shard_map.77 = (f32[1,36]{1,0:T(1,128)}, f32[1,6]{1,0:T(1,128)}, f32[8,36]{1,0:T(8,128)}) custom-call(f32[16,128]{1,0:T(8,128)S(1)} %shard_map.76.sums_ref), custom_call_target="tpu_custom_call" | custom-call | tf_op jit(solution)/shard_map/pallas_call | solution.py:227

commit v3 on v2

--- a/solution.py
+++ b/solution.py
@@ -35,8 +35,6 @@
     barrier = pltpu.get_barrier_semaphore()
     for k in range(1, rounds + 1):
         pl.semaphore_signal(barrier, inc=1, device_id=(up(k), rep), device_id_type=MESH)
-        for half in range(2):
-            pl.semaphore_signal(barrier, inc=1, device_id=(down(k), half), device_id_type=MESH)
     pl.semaphore_signal(barrier, inc=1, device_id=(me, 1 - rep), device_id_type=MESH)
 
     loads = [
@@ -58,11 +56,11 @@
                 p_send[k, c, pl.ds(j, 1), :] = pts[c, pl.ds(block, 1), :]
         a_send[k] = jnp.full((1, LANES), act[0, k], jnp.int32)
 
-    pl.semaphore_wait(barrier, 3 * rounds + 1)
+    pl.semaphore_wait(barrier, rounds + 1)
 
     sends = []
     order = list(range(rounds))
-    for k in reversed(order):
+    for k in order:
         to = (down(k + 1), rep)
         for source, target, ssem, rsem in (
             (tgt.at[k], i_recv.at[k], i_ssem.at[k], i_rsem.at[k]),
@@ -100,7 +98,7 @@
         )
 
     def one_pair(step, tsum):
-        k = rounds - 1 - step
+        k = step
         inbound(k, tgt, i_recv, i_ssem, i_rsem).wait_recv()
         index = i_recv[k]
         row_of = lax.shift_right_logical(index, 7)

time: 29.4 us -> 27.6 us (0.939); the launches traced: 29.3 us -> 27.2 us
  Pallas kernels: 28.6 us -> 26.5 us
    pallas_call x1, Pallas kernels: 28 us -> 25.9 us  [body(): pl.pallas_call(functools.partial(kernel, n_blk, rounds, nslots, npts), ou...]
where the time goes in v3:
time: 27.6 us; the launch traced here: 27.2 us
  Pallas kernels  26.5 us (96%)
  between operations  0.64 us (2%)
    pallas_call x1, Pallas kernels, body(): pl.pallas_call(functools.partial(kernel, n_blk, rounds, nslots, npts), ou...  25.9 us
    pallas_call x1, Pallas kernels, body(): pl.pallas_call(functools.partial(finish, rounds, total_slots), out_shape=...  0.67 us

profile of v3, /device:TPU:1, one launch (start us, length us, event | category | flops | bytes accessed | tf_op | source)
XLA Modules:
  0.0 27.2 jit_solution(1136719659032655775)
XLA Ops:
  0.6 25.9 %shard_map.76.sums_ref = f32[16,128]{1,0:T(8,128)S(1)} custom-call(f32[3,64,128]{2,1,0:T(8,128)} %bitcast.8, f32[3,64,128]{2,1,0:T(8,128)} %bitcast.9, s32[8,8]{1,0:T(8,128)} %bitcast.11, s32[8,8,128]{2,1,0:T(8,128)} %bitcast.10, s32[1,8]{1,0:T(1,128)} %bitcast.12), custom_call_target="tpu_custom_call" | custom-call | tf_op jit(solution)/shard_map/pallas_call | solution.py:189
  26.5 0.7 %shard_map.77 = (f32[1,36]{1,0:T(1,128)}, f32[1,6]{1,0:T(1,128)}, f32[8,36]{1,0:T(8,128)}) custom-call(f32[16,128]{1,0:T(8,128)S(1)} %shard_map.76.sums_ref), custom_call_target="tpu_custom_call" | custom-call | tf_op jit(solution)/shard_map/pallas_call | solution.py:225

commit v4 on v3

v4 whole, which is shorter than its diff:
```python
import functools

import jax
import jax.numpy as jnp
from jax import lax
from jax.experimental import pallas as pl
from jax.experimental.pallas import tpu as pltpu
from jax.sharding import PartitionSpec as P

MESH = pl.DeviceIdType.MESH
LANES = 128
SIDE = 4
ENTRIES = [(i, j) for i in range(6) for j in range(i, 6)]


def kernel(
    n_blk, rounds, nslots, npts, side,
    pts_hbm, nrm_hbm, src_hbm, tgt_hbm, act_hbm,
    out_ref,
    tab, tgt, src, act,
    p_send, a_send, i_recv, p_recv, a_recv,
    prods, r_send, r_recv, t_send, t_recv,
    local_sem, i_ssem, i_rsem, p_ssem, p_rsem, a_ssem, a_rsem,
    r_ssem, r_rsem, t_ssem, t_rsem, f_ssem, late_sem,
):
    me = lax.axis_index("blk")
    rep = lax.axis_index("rep")
    rows = npts // LANES
    order = range(rounds)
    is_late = me >= n_blk - rounds
    is_helper = me < rounds
    is_own = me < side
    late_of_me = me + n_blk - jnp.where(is_own, side, rounds + side)
    plane = side * side
    is_post = jnp.logical_and(me >= plane - rounds, me < plane)
    helper_of_post = me - jnp.where(me < plane - side, side, rounds + side)

    def near(k):
        return me + k < n_blk

    def helps(k):
        return jnp.logical_and(is_helper, late_of_me + k >= n_blk)

    def helped(k):
        return late_of_me + k - n_blk

    def host(k):
        return me - k + jnp.where(me >= k, 0, jnp.where(me >= k - side, side, rounds + side))

    def copy_to(source, target, ssem, rsem, blk, core):
        return pltpu.make_async_remote_copy(
            src_ref=source, dst_ref=target, send_sem=ssem, recv_sem=rsem,
            device_id=(blk, core), device_id_type=MESH,
        )

    loads = [
        pltpu.make_async_copy(src_hbm, src, local_sem.at[0]),
        pltpu.make_async_copy(act_hbm, act, local_sem.at[1]),
        pltpu.make_async_copy(pts_hbm, tab.at[0], local_sem.at[2]),
        pltpu.make_async_copy(tgt_hbm, tgt, local_sem.at[3]),
        pltpu.make_async_copy(nrm_hbm, tab.at[1], local_sem.at[4]),
    ]

    barrier = pltpu.get_barrier_semaphore()

    def greet(blk, core):
        pl.semaphore_signal(barrier, inc=1, device_id=(blk, core), device_id_type=MESH)

    for load in loads:
        load.start()

    @pl.when(is_late)
    def _():
        greet(me - n_blk + plane, rep)

    @pl.when(is_helper)
    def _():
        greet(late_of_me - n_blk + plane, rep)

    greet(me, 1 - rep)
    for k in range(1, rounds + 1):
        @pl.when(near(k))
        def _():
            greet(me + k, rep)

        if k != side:
            @pl.when(helps(k))
            def _():
                greet(helped(k), rep)

    @pl.when(is_post)
    def _():
        pl.semaphore_wait(barrier, rounds + 3)
        pl.semaphore_signal(late_sem, inc=1, device_id=(helper_of_post, rep), device_id_type=MESH)

    for load in loads:
        load.wait()

    for k in order:
        for j in range(nslots):
            block = src[k, j]
            for c in range(3):
                p_send[k, c, pl.ds(j, 1), :] = tab[0, c, pl.ds(block, 1), :]
        a_send[k] = jnp.full((1, LANES), act[0, k], jnp.int32)

    @pl.when(jnp.logical_not(is_post))
    def _():
        pl.semaphore_wait(barrier, rounds + jnp.where(is_own, 0, 1))

    def outbound(k):
        blk = host(k + 1)
        slot = k + jnp.where(me < k + 1, rounds, 0)
        return [
            copy_to(tgt.at[k], i_recv.at[slot], i_ssem.at[k], i_rsem.at[slot], blk, rep),
            copy_to(a_send.at[k], a_recv.at[slot], a_ssem.at[k], a_rsem.at[slot], blk, rep),
            copy_to(p_send.at[k], p_recv.at[slot], p_ssem.at[k], p_rsem.at[slot], blk, rep),
        ]

    def arrival(source, target, ssem, rsem, k, slot):
        copy_to(source.at[k], target.at[slot], ssem.at[k], rsem.at[slot], host(k + 1), rep).wait_recv()

    for k in order:
        @pl.when(jnp.logical_not(jnp.logical_and(is_own, k + 1 == side)))
        def _():
            for copy in outbound(k):
                copy.start()

    sub = lax.broadcasted_iota(jnp.int32, (nslots, LANES), 0)
    lane = lax.broadcasted_iota(jnp.int32, (nslots, LANES), 1)
    slot_of = sub + rep * nslots
    li, lj = lane // 6, lane % 6
    lo, hi = jnp.minimum(li, lj), jnp.maximum(li, lj)
    entry_of = jnp.where(
        lane < 36, lo * 6 - (lo * (lo - 1)) // 2 + hi - lo,
        jnp.where(lane < 42, lane - 36 + 21, -1),
    )

    def forwards(k):
        slot = k + rounds
        parts = ((tgt, i_recv, i_rsem), (a_send, a_recv, a_rsem), (p_send, p_recv, p_rsem))
        return [
            copy_to(
                mine.at[k] if k + 1 == side else ref.at[slot],
                ref.at[k], f_ssem.at[e, k], rsem.at[k], late_of_me, rep,
            )
            for e, (mine, ref, rsem) in enumerate(parts)
        ]

    @pl.when(is_helper)
    def _():
        pl.semaphore_wait(late_sem, 1)
        for step in order:
            for k in order:
                @pl.when(jnp.logical_and(helps(k + 1), helped(k + 1) == step // 2 + step % 2 * side))
                def _():
                    if k + 1 != side:
                        arrival(tgt, i_recv, i_ssem, i_rsem, k, k + rounds)
                        arrival(a_send, a_recv, a_ssem, a_rsem, k, k + rounds)
                        arrival(p_send, p_recv, p_ssem, p_rsem, k, k + rounds)
                    for copy in forwards(k):
                        copy.start()

    def returned(k, half):
        return copy_to(
            r_send.at[k], r_recv.at[rep, k], r_ssem.at[half, k], r_rsem.at[rep, k],
            lax.rem(me + k + 1, n_blk), half,
        )

    def turn(step):
        source = jnp.where(me >= n_blk - 2, (step % 2) * side + step // 2, step)
        return jnp.where(is_late, lax.rem(source + n_blk - 1 - me, rounds), step)

    def gather(k):
        arrival(tgt, i_recv, i_ssem, i_rsem, k, k)
        index = i_recv[k]
        row_of = lax.shift_right_logical(index, 7)
        lane_of = lax.bitwise_and(index, LANES - 1)
        acc = [jnp.zeros((nslots, LANES), jnp.float32)] * 6
        for row in range(rows):
            here = row_of == row
            for e in range(6):
                line = jnp.broadcast_to(tab[e // 3, e % 3, row : row + 1, :], (nslots, LANES))
                got = jnp.take_along_axis(line, lane_of, axis=1, mode="promise_in_bounds")
                acc[e] = jnp.where(here, got, acc[e])
        return tuple(acc)

    def await_points(k):
        arrival(a_send, a_recv, a_ssem, a_rsem, k, k)
        arrival(p_send, p_recv, p_ssem, p_rsem, k, k)

    def gram(k, picked):
        q0, q1, q2, n0, n1, n2 = picked
        live = (slot_of < a_recv[k]).astype(jnp.float32)
        p0, p1, p2 = p_recv[k, 0], p_recv[k, 1], p_recv[k, 2]
        resid = n0 * (p0 - q0) + n1 * (p1 - q1) + n2 * (p2 - q2)
        weight = live / (1.0 + resid * resid)
        jacob = [p1 * n2 - p2 * n1, p2 * n0 - p0 * n2, p0 * n1 - p1 * n0, n0, n1, n2]
        scaled = [weight * entry for entry in jacob]
        for e, (i, j) in enumerate(ENTRIES):
            prods[pl.ds(e * 8, 8), :] = scaled[i] * jacob[j]
        for i in range(6):
            prods[pl.ds((21 + i) * 8, 8), :] = scaled[i] * resid
        spread = jnp.zeros((8, LANES), jnp.float32)
        for g in range(4):
            some = prods[pl.ds(g * 64, 8, stride=8), :]
            for t in range(1, 8):
                some = some + prods[pl.ds(g * 64 + t, 8, stride=8), :]
            whole = jnp.sum(some, axis=1, keepdims=True)
            spread = spread + jnp.where(entry_of == sub + g * 8, whole, 0.0)
        line = jnp.sum(spread, axis=0, keepdims=True)
        r_send[k] = line
        return line

    def give_back(k):
        for half in range(2):
            returned(k, half).start()

    def one_step(step, carry):
        picked, tsum = carry[:6], carry[6]
        before, k = turn(step - 1), turn(step)
        await_points(before)
        arrived = gather(k)
        line = gram(before, picked)
        give_back(before)
        return arrived + (tsum + line,)

    first = gather(turn(0))
    carry = lax.fori_loop(1, rounds, one_step, first + (jnp.zeros((1, LANES), jnp.float32),))
    last = turn(rounds - 1)
    await_points(last)
    line = gram(last, carry[:6])
    give_back(last)
    t_send[...] = carry[6] + line

    exchange = copy_to(t_send, t_recv, t_ssem, t_rsem, me, 1 - rep)
    exchange.start()

    source_sum = jnp.zeros((1, LANES), jnp.float32)
    for k in order:
        for half in range(2):
            copy_to(
                r_send.at[k], r_recv.at[half, k], r_ssem.at[half, k], r_rsem.at[half, k], host(k + 1), half
            ).wait_recv()
        both = r_recv[0, k] + r_recv[1, k]
        out_ref[pl.ds(k, 1), :] = both
        source_sum = source_sum + both
    exchange.wait_recv()
    target_sum = t_send[...] + t_recv[...]
    lane1 = lax.broadcasted_iota(jnp.int32, (1, LANES), 1)
    out_ref[pl.ds(rounds, 1), :] = source_sum + jnp.where(lane1 < 36, target_sum, -target_sum)

    for k in order:
        @pl.when(jnp.logical_not(jnp.logical_and(is_own, k + 1 == side)))
        def _():
            for copy in outbound(k):
                copy.wait_send()

    for k in order:
        for half in range(2):
            returned(k, half).wait_send()
    exchange.wait_send()

    @pl.when(is_helper)
    def _():
        for k in order:
            @pl.when(helps(k + 1))
            def _():
                for copy in forwards(k):
                    copy.wait_send()


def finish(rounds, total_slots, sums_ref, diag_ref, grad_ref, pair_ref):
    pair_ref[...] = sums_ref[:rounds, :36] * (1.0 / total_slots)
    total = sums_ref[rounds : rounds + 1] * (1.0 / (total_slots * 2.0 * rounds))
    diag_ref[...] = total[:, :36]
    grad_ref[...] = total[:, 36:42]


def solution(mesh):
    n_blk = mesh.shape["blk"]

    def body(points, normals, src_block, tgt_index, active):
        npts = points.shape[2]
        rounds, nslots = src_block.shape[0], src_block.shape[3]
        rows = npts // LANES
        f32, i32 = jnp.float32, jnp.int32
        dma = pltpu.SemaphoreType.DMA
        total_slots = 2 * nslots * LANES
        sums = pl.pallas_call(
            functools.partial(kernel, n_blk, rounds, nslots, npts, SIDE),
            out_shape=jax.ShapeDtypeStruct((rounds + 8, LANES), f32),
            in_specs=[pl.BlockSpec(memory_space=pl.ANY)] * 5,
            out_specs=pl.BlockSpec(memory_space=pltpu.VMEM),
            scratch_shapes=[
                pltpu.VMEM((2, 3, rows, LANES), f32),
                pltpu.VMEM((rounds, nslots, LANES), i32),
                pltpu.SMEM((rounds, nslots), i32),
                pltpu.SMEM((1, rounds), i32),
                pltpu.VMEM((rounds, 3, nslots, LANES), f32),
                pltpu.VMEM((rounds, 1, LANES), i32),
                pltpu.VMEM((2 * rounds, nslots, LANES), i32),
                pltpu.VMEM((2 * rounds, 3, nslots, LANES), f32),
                pltpu.VMEM((2 * rounds, 1, LANES), i32),
                pltpu.VMEM((256, LANES), f32),
                pltpu.VMEM((rounds, 1, LANES), f32),
                pltpu.VMEM((2, rounds, 1, LANES), f32),
                pltpu.VMEM((1, LANES), f32),
                pltpu.VMEM((1, LANES), f32),
                dma((5,)),
                dma((rounds,)), dma((2 * rounds,)),
                dma((rounds,)), dma((2 * rounds,)),
                dma((rounds,)), dma((2 * rounds,)),
                dma((2, rounds)), dma((2, rounds)),
                dma, dma, dma((3, rounds)), pltpu.SemaphoreType.REGULAR,
            ],
            compiler_params=pltpu.CompilerParams(collective_id=0, has_side_effects=True, vmem_limit_bytes=8 * 1024 * 1024),
        )(
            pltpu.with_memory_space_constraint(points.reshape(3, rows, LANES), pltpu.HBM),
            pltpu.with_memory_space_constraint(normals.reshape(3, rows, LANES), pltpu.HBM),
            pltpu.with_memory_space_constraint(src_block.reshape(rounds, nslots), pltpu.HBM),
            pltpu.with_memory_space_constraint(tgt_index.reshape(rounds, nslots, LANES), pltpu.HBM),
            pltpu.with_memory_space_constraint(active.reshape(1, rounds), pltpu.HBM),
        )
        diag, grad, pair = pl.pallas_call(
            functools.partial(finish, rounds, total_slots),
            out_shape=(
                jax.ShapeDtypeStruct((1, 36), f32),
                jax.ShapeDtypeStruct((1, 6), f32),
                jax.ShapeDtypeStruct((rounds, 36), f32),
            ),
            compiler_params=pltpu.CompilerParams(vmem_limit_bytes=1024 * 1024),
        )(sums)
        return diag, grad, pair.reshape(rounds, 1, 1, 36)

    return jax.shard_map(
        body,
        mesh=mesh,
        in_specs=(
            P("blk", None, None),
            P("blk", None, None),
            P(None, "blk", None, "rep"),
            P(None, "blk", None, "rep", None),
            P(None, "blk", None),
        ),
        out_specs=(P("blk", None), P("blk", None), P(None, "blk", None, None)),
        check_vma=False,
    )
```

time: 27.6 us -> 24.4 us (0.88); the launches traced: 27.2 us -> 24.3 us
  Pallas kernels: 26.5 us -> 23.6 us
    pallas_call x1, Pallas kernels: 25.9 us -> 23 us  [body(): pl.pallas_call(functools.partial(kernel, n_blk, rounds, nslots, npts, SID...]
where the time goes in v4:
time: 24.4 us; the launch traced here: 24.3 us
  Pallas kernels  23.6 us (97%)
  between operations  0.64 us (3%)
    pallas_call x1, Pallas kernels, body(): pl.pallas_call(functools.partial(kernel, n_blk, rounds, nslots, npts, SID...  23 us
    pallas_call x1, Pallas kernels, body(): pl.pallas_call(functools.partial(finish, rounds, total_slots), out_shape=...  0.67 us

profile of v4, /device:TPU:1, one launch (start us, length us, event | category | flops | bytes accessed | tf_op | source)
XLA Modules:
  0.0 24.3 jit_solution(1906646184233172557)
XLA Ops:
  0.6 23.0 %shard_map.76.sums_ref = f32[16,128]{1,0:T(8,128)S(1)} custom-call(f32[3,64,128]{2,1,0:T(8,128)} %bitcast.8, f32[3,64,128]{2,1,0:T(8,128)} %bitcast.9, s32[8,8]{1,0:T(8,128)} %bitcast.11, s32[8,8,128]{2,1,0:T(8,128)} %bitcast.10, s32[1,8]{1,0:T(1,128)} %bitcast.12), custom_call_target="tpu_custom_call" | custom-call | tf_op jit(solution)/shard_map/pallas_call | solution.py:289
  23.6 0.7 %shard_map.77 = (f32[1,36]{1,0:T(1,128)}, f32[1,6]{1,0:T(1,128)}, f32[8,36]{1,0:T(8,128)}) custom-call(f32[16,128]{1,0:T(8,128)S(1)} %shard_map.76.sums_ref), custom_call_target="tpu_custom_call" | custom-call | tf_op jit(solution)/shard_map/pallas_call | solution.py:324

commit v5 on v4

--- a/solution.py
+++ b/solution.py
@@ -18,15 +18,16 @@
     pts_hbm, nrm_hbm, src_hbm, tgt_hbm, act_hbm,
     out_ref,
     tab, tgt, src, act,
-    p_send, a_send, i_recv, p_recv, a_recv,
+    m_send, m_recv,
     prods, r_send, r_recv, t_send, t_recv,
-    local_sem, i_ssem, i_rsem, p_ssem, p_rsem, a_ssem, a_rsem,
+    local_sem, m_ssem, m_rsem,
     r_ssem, r_rsem, t_ssem, t_rsem, f_ssem, late_sem,
 ):
     me = lax.axis_index("blk")
     rep = lax.axis_index("rep")
     rows = npts // LANES
     order = range(rounds)
+    far_first = (6, 7, 5, 2, 8, 3, 1, 4)
     is_late = me >= n_blk - rounds
     is_helper = me < rounds
     is_own = me < side
@@ -66,19 +67,19 @@
     def greet(blk, core):
         pl.semaphore_signal(barrier, inc=1, device_id=(blk, core), device_id_type=MESH)
 
+    @pl.when(is_late)
+    def _():
+        greet(me - n_blk + plane, rep)
+
     for load in loads:
         load.start()
 
-    @pl.when(is_late)
-    def _():
-        greet(me - n_blk + plane, rep)
-
     @pl.when(is_helper)
     def _():
         greet(late_of_me - n_blk + plane, rep)
 
     greet(me, 1 - rep)
-    for k in range(1, rounds + 1):
+    for k in far_first:
         @pl.when(near(k))
         def _():
             greet(me + k, rep)
@@ -100,30 +101,25 @@
         for j in range(nslots):
             block = src[k, j]
             for c in range(3):
-                p_send[k, c, pl.ds(j, 1), :] = tab[0, c, pl.ds(block, 1), :]
-        a_send[k] = jnp.full((1, LANES), act[0, k], jnp.int32)
+                m_send[k, c, pl.ds(j, 1), :] = tab[0, c, pl.ds(block, 1), :]
+        m_send[k, 3] = tgt[k].astype(jnp.float32)
+        m_send[k, 4] = jnp.full((nslots, LANES), act[0, k].astype(jnp.float32), jnp.float32)
 
     @pl.when(jnp.logical_not(is_post))
     def _():
         pl.semaphore_wait(barrier, rounds + jnp.where(is_own, 0, 1))
 
     def outbound(k):
-        blk = host(k + 1)
         slot = k + jnp.where(me < k + 1, rounds, 0)
-        return [
-            copy_to(tgt.at[k], i_recv.at[slot], i_ssem.at[k], i_rsem.at[slot], blk, rep),
-            copy_to(a_send.at[k], a_recv.at[slot], a_ssem.at[k], a_rsem.at[slot], blk, rep),
-            copy_to(p_send.at[k], p_recv.at[slot], p_ssem.at[k], p_rsem.at[slot], blk, rep),
-        ]
-
-    def arrival(source, target, ssem, rsem, k, slot):
-        copy_to(source.at[k], target.at[slot], ssem.at[k], rsem.at[slot], host(k + 1), rep).wait_recv()
-
-    for k in order:
+        return copy_to(m_send.at[k], m_recv.at[slot], m_ssem.at[k], m_rsem.at[slot], host(k + 1), rep)
+
+    def arrival(k, slot):
+        copy_to(m_send.at[k], m_recv.at[slot], m_ssem.at[k], m_rsem.at[slot], host(k + 1), rep).wait_recv()
+
+    for k in (far - 1 for far in far_first):
         @pl.when(jnp.logical_not(jnp.logical_and(is_own, k + 1 == side)))
         def _():
-            for copy in outbound(k):
-                copy.start()
+            outbound(k).start()
 
     sub = lax.broadcasted_iota(jnp.int32, (nslots, LANES), 0)
     lane = lax.broadcasted_iota(jnp.int32, (nslots, LANES), 1)
@@ -135,16 +131,9 @@
         jnp.where(lane < 42, lane - 36 + 21, -1),
     )
 
-    def forwards(k):
-        slot = k + rounds
-        parts = ((tgt, i_recv, i_rsem), (a_send, a_recv, a_rsem), (p_send, p_recv, p_rsem))
-        return [
-            copy_to(
-                mine.at[k] if k + 1 == side else ref.at[slot],
-                ref.at[k], f_ssem.at[e, k], rsem.at[k], late_of_me, rep,
-            )
-            for e, (mine, ref, rsem) in enumerate(parts)
-        ]
+    def forward(k):
+        source = m_send.at[k] if k + 1 == side else m_recv.at[k + rounds]
+        return copy_to(source, m_recv.at[k], f_ssem.at[k], m_rsem.at[k], late_of_me, rep)
 
     @pl.when(is_helper)
     def _():
@@ -154,11 +143,8 @@
                 @pl.when(jnp.logical_and(helps(k + 1), helped(k + 1) == step // 2 + step % 2 * side))
                 def _():
                     if k + 1 != side:
-                        arrival(tgt, i_recv, i_ssem, i_rsem, k, k + rounds)
-                        arrival(a_send, a_recv, a_ssem, a_rsem, k, k + rounds)
-                        arrival(p_send, p_recv, p_ssem, p_rsem, k, k + rounds)
-                    for copy in forwards(k):
-                        copy.start()
+                        arrival(k, k + rounds)
+                    forward(k).start()
 
     def returned(k, half):
         return copy_to(
@@ -168,11 +154,14 @@
 
     def turn(step):
         source = jnp.where(me >= n_blk - 2, (step % 2) * side + step // 2, step)
-        return jnp.where(is_late, lax.rem(source + n_blk - 1 - me, rounds), step)
+        usual = step * 0
+        for place, far in enumerate(far_first):
+            usual = jnp.where(step == place, far - 1, usual)
+        return jnp.where(is_late, lax.rem(source + n_blk - 1 - me, rounds), usual)
 
     def gather(k):
-        arrival(tgt, i_recv, i_ssem, i_rsem, k, k)
-        index = i_recv[k]
+        arrival(k, k)
+        index = m_recv[k, 3].astype(jnp.int32)
         row_of = lax.shift_right_logical(index, 7)
         lane_of = lax.bitwise_and(index, LANES - 1)
         acc = [jnp.zeros((nslots, LANES), jnp.float32)] * 6
@@ -184,14 +173,10 @@
                 acc[e] = jnp.where(here, got, acc[e])
         return tuple(acc)
 
-    def await_points(k):
-        arrival(a_send, a_recv, a_ssem, a_rsem, k, k)
-        arrival(p_send, p_recv, p_ssem, p_rsem, k, k)
-
     def gram(k, picked):
         q0, q1, q2, n0, n1, n2 = picked
-        live = (slot_of < a_recv[k]).astype(jnp.float32)
-        p0, p1, p2 = p_recv[k, 0], p_recv[k, 1], p_recv[k, 2]
+        live = (slot_of < m_recv[k, 4].astype(jnp.int32)).astype(jnp.float32)
+        p0, p1, p2 = m_recv[k, 0], m_recv[k, 1], m_recv[k, 2]
         resid = n0 * (p0 - q0) + n1 * (p1 - q1) + n2 * (p2 - q2)
         weight = live / (1.0 + resid * resid)
         jacob = [p1 * n2 - p2 * n1, p2 * n0 - p0 * n2, p0 * n1 - p1 * n0, n0, n1, n2]
@@ -200,13 +185,19 @@
             prods[pl.ds(e * 8, 8), :] = scaled[i] * jacob[j]
         for i in range(6):
             prods[pl.ds((21 + i) * 8, 8), :] = scaled[i] * resid
-        spread = jnp.zeros((8, LANES), jnp.float32)
+        parts = []
         for g in range(4):
             some = prods[pl.ds(g * 64, 8, stride=8), :]
             for t in range(1, 8):
                 some = some + prods[pl.ds(g * 64 + t, 8, stride=8), :]
-            whole = jnp.sum(some, axis=1, keepdims=True)
-            spread = spread + jnp.where(entry_of == sub + g * 8, whole, 0.0)
+            parts.append(some)
+        whole = jnp.dot(
+            jnp.concatenate(parts, axis=0), jnp.ones((LANES, LANES), jnp.float32),
+            precision=lax.Precision.HIGHEST, preferred_element_type=jnp.float32,
+        )
+        spread = jnp.zeros((8, LANES), jnp.float32)
+        for g in range(4):
+            spread = spread + jnp.where(entry_of == sub + g * 8, whole[g * 8 : g * 8 + 8], 0.0)
         line = jnp.sum(spread, axis=0, keepdims=True)
         r_send[k] = line
         return line
@@ -218,7 +209,6 @@
     def one_step(step, carry):
         picked, tsum = carry[:6], carry[6]
         before, k = turn(step - 1), turn(step)
-        await_points(before)
         arrived = gather(k)
         line = gram(before, picked)
         give_back(before)
@@ -227,7 +217,6 @@
     first = gather(turn(0))
     carry = lax.fori_loop(1, rounds, one_step, first + (jnp.zeros((1, LANES), jnp.float32),))
     last = turn(rounds - 1)
-    await_points(last)
     line = gram(last, carry[:6])
     give_back(last)
     t_send[...] = carry[6] + line
@@ -252,8 +241,7 @@
     for k in order:
         @pl.when(jnp.logical_not(jnp.logical_and(is_own, k + 1 == side)))
         def _():
-            for copy in outbound(k):
-                copy.wait_send()
+            outbound(k).wait_send()
 
     for k in order:
         for half in range(2):
@@ -265,8 +253,7 @@
         for k in order:
             @pl.when(helps(k + 1))
             def _():
-                for copy in forwards(k):
-                    copy.wait_send()
+                forward(k).wait_send()
 
 
 def finish(rounds, total_slots, sums_ref, diag_ref, grad_ref, pair_ref):
@@ -296,11 +283,8 @@
                 pltpu.VMEM((rounds, nslots, LANES), i32),
                 pltpu.SMEM((rounds, nslots), i32),
                 pltpu.SMEM((1, rounds), i32),
-                pltpu.VMEM((rounds, 3, nslots, LANES), f32),
-                pltpu.VMEM((rounds, 1, LANES), i32),
-                pltpu.VMEM((2 * rounds, nslots, LANES), i32),
-                pltpu.VMEM((2 * rounds, 3, nslots, LANES), f32),
-                pltpu.VMEM((2 * rounds, 1, LANES), i32),
+                pltpu.VMEM((rounds, 5, nslots, LANES), f32),
+                pltpu.VMEM((2 * rounds, 5, nslots, LANES), f32),
                 pltpu.VMEM((256, LANES), f32),
                 pltpu.VMEM((rounds, 1, LANES), f32),
                 pltpu.VMEM((2, rounds, 1, LANES), f32),
@@ -308,10 +292,8 @@
                 pltpu.VMEM((1, LANES), f32),
                 dma((5,)),
                 dma((rounds,)), dma((2 * rounds,)),
-                dma((rounds,)), dma((2 * rounds,)),
-                dma((rounds,)), dma((2 * rounds,)),
                 dma((2, rounds)), dma((2, rounds)),
-                dma, dma, dma((3, rounds)), pltpu.SemaphoreType.REGULAR,
+                dma, dma, dma((rounds,)), pltpu.SemaphoreType.REGULAR,
             ],
             compiler_params=pltpu.CompilerParams(collective_id=0, has_side_effects=True, vmem_limit_bytes=8 * 1024 * 1024),
         )(

time: 24.4 us -> 24.1 us (0.988)
  Pallas kernels: 23.6 us -> 23.3 us
    pallas_call x1, Pallas kernels: 23 us -> 22.6 us  [body(): pl.pallas_call(functools.partial(kernel, n_blk, rounds, nslots, npts, SID...]
where the time goes in v5:
time: 24.1 us; the launch traced here: 23.9 us
  Pallas kernels  23.3 us (97%)
  between operations  0.64 us (3%)
    pallas_call x1, Pallas kernels, body(): pl.pallas_call(functools.partial(kernel, n_blk, rounds, nslots, npts, SID...  22.6 us
    pallas_call x1, Pallas kernels, body(): pl.pallas_call(functools.partial(finish, rounds, total_slots), out_shape=...  0.67 us

profile of v5, /device:TPU:1, one launch (start us, length us, event | category | flops | bytes accessed | tf_op | source)
XLA Modules:
  0.0 23.9 jit_solution(15807843885905633393)
XLA Ops:
  0.6 22.6 %shard_map.76.sums_ref = f32[16,128]{1,0:T(8,128)S(1)} custom-call(f32[3,64,128]{2,1,0:T(8,128)} %bitcast.8, f32[3,64,128]{2,1,0:T(8,128)} %bitcast.9, s32[8,8]{1,0:T(8,128)} %bitcast.11, s32[8,8,128]{2,1,0:T(8,128)} %bitcast.10, s32[1,8]{1,0:T(1,128)} %bitcast.12), custom_call_target="tpu_custom_call" | custom-call | tf_op jit(solution)/shard_map/pallas_call | solution.py:276
  23.3 0.7 %shard_map.77 = (f32[1,36]{1,0:T(1,128)}, f32[1,6]{1,0:T(1,128)}, f32[8,36]{1,0:T(8,128)}) custom-call(f32[16,128]{1,0:T(8,128)S(1)} %shard_map.76.sums_ref), custom_call_target="tpu_custom_call" | custom-call | tf_op jit(solution)/shard_map/pallas_call | solution.py:306

commit v6 on v5

--- a/solution.py
+++ b/solution.py
@@ -18,7 +18,7 @@
     pts_hbm, nrm_hbm, src_hbm, tgt_hbm, act_hbm,
     out_ref,
     tab, tgt, src, act,
-    m_send, m_recv,
+    m_send, m_recv, split, stage,
     prods, r_send, r_recv, t_send, t_recv,
     local_sem, m_ssem, m_rsem,
     r_ssem, r_rsem, t_ssem, t_rsem, f_ssem, late_sem,
@@ -121,6 +121,14 @@
         def _():
             outbound(k).start()
 
+    for c in range(3):
+        normal = jnp.concatenate(
+            [tab[1, c, pl.ds(odd, rows // 2, stride=2), :] for odd in range(2)], axis=1
+        )
+        top = normal.astype(jnp.bfloat16)
+        split[pl.ds(c * rows, rows // 2), :] = top
+        split[pl.ds(c * rows + rows // 2, rows // 2), :] = (normal - top.astype(jnp.float32)).astype(jnp.bfloat16)
+
     sub = lax.broadcasted_iota(jnp.int32, (nslots, LANES), 0)
     lane = lax.broadcasted_iota(jnp.int32, (nslots, LANES), 1)
     slot_of = sub + rep * nslots
@@ -159,18 +167,42 @@
             usual = jnp.where(step == place, far - 1, usual)
         return jnp.where(is_late, lax.rem(source + n_blk - 1 - me, rounds), usual)
 
+    half = rows // 2
+    row_pair = lax.broadcasted_iota(jnp.int32, (half, LANES), 0)
+    in_pair = lax.broadcasted_iota(jnp.int32, (2 * LANES, LANES), 0).astype(jnp.float32).astype(jnp.bfloat16)
+    one, none = (jnp.full((2 * LANES, LANES), value, jnp.bfloat16) for value in (1.0, 0.0))
+
     def gather(k):
         arrival(k, k)
         index = m_recv[k, 3].astype(jnp.int32)
         row_of = lax.shift_right_logical(index, 7)
         lane_of = lax.bitwise_and(index, LANES - 1)
-        acc = [jnp.zeros((nslots, LANES), jnp.float32)] * 6
+        pair_of = lax.shift_right_logical(index, 8)
+        spot = lax.bitwise_and(index, 2 * LANES - 1).astype(jnp.float32)
+        hot = []
+        for j in range(nslots):
+            here = jnp.broadcast_to(spot[j : j + 1].astype(jnp.bfloat16), (2 * LANES, LANES))
+            hot.append(jnp.where(in_pair == here, one, none))
+        chosen = jnp.dot(split[...], jnp.concatenate(hot, axis=1), preferred_element_type=jnp.float32)
+        acc = [jnp.zeros((nslots, LANES), jnp.float32)] * 3
         for row in range(rows):
             here = row_of == row
-            for e in range(6):
-                line = jnp.broadcast_to(tab[e // 3, e % 3, row : row + 1, :], (nslots, LANES))
+            for c in range(3):
+                line = jnp.broadcast_to(tab[0, c, row : row + 1, :], (nslots, LANES))
                 got = jnp.take_along_axis(line, lane_of, axis=1, mode="promise_in_bounds")
-                acc[e] = jnp.where(here, got, acc[e])
+                acc[c] = jnp.where(here, got, acc[c])
+        for j in range(nslots):
+            here = row_pair == jnp.broadcast_to(pair_of[j : j + 1], (half, LANES))
+            for c in range(3):
+                block = chosen[c * rows : (c + 1) * rows, j * LANES : (j + 1) * LANES]
+                found = jnp.where(here, block[:half] + block[half:], 0.0)
+                found = sum(found[i : i + 8] for i in range(8, half, 8)) + found[:8]
+                stage[pl.ds((c * nslots + j) * 8, 8), :] = found
+        for c in range(3):
+            total = stage[pl.ds(c * nslots * 8, nslots, stride=8), :]
+            for i in range(1, 8):
+                total = total + stage[pl.ds(c * nslots * 8 + i, nslots, stride=8), :]
+            acc.append(total)
         return tuple(acc)
 
     def gram(k, picked):
@@ -214,8 +246,9 @@
         give_back(before)
         return arrived + (tsum + line,)
 
-    first = gather(turn(0))
-    carry = lax.fori_loop(1, rounds, one_step, first + (jnp.zeros((1, LANES), jnp.float32),))
+    opening = gram(turn(0), gather(turn(0)))
+    give_back(turn(0))
+    carry = lax.fori_loop(2, rounds, one_step, gather(turn(1)) + (opening,))
     last = turn(rounds - 1)
     line = gram(last, carry[:6])
     give_back(last)
@@ -285,6 +318,8 @@
                 pltpu.SMEM((1, rounds), i32),
                 pltpu.VMEM((rounds, 5, nslots, LANES), f32),
                 pltpu.VMEM((2 * rounds, 5, nslots, LANES), f32),
+                pltpu.VMEM((3 * rows, 2 * LANES), jnp.bfloat16),
+                pltpu.VMEM((3 * nslots * 8, LANES), f32),
                 pltpu.VMEM((256, LANES), f32),
                 pltpu.VMEM((rounds, 1, LANES), f32),
                 pltpu.VMEM((2, rounds, 1, LANES), f32),

time: 24.1 us -> 23.7 us (0.983)
  Pallas kernels: 23.3 us -> 22.9 us
    pallas_call x1, Pallas kernels: 22.6 us -> 22.3 us  [body(): pl.pallas_call(functools.partial(kernel, n_blk, rounds, nslots, npts, SID...]
where the time goes in v6:
time: 23.7 us; the launch traced here: 23.6 us
  Pallas kernels  22.9 us (97%)
  between operations  0.64 us (3%)
    pallas_call x1, Pallas kernels, body(): pl.pallas_call(functools.partial(kernel, n_blk, rounds, nslots, npts, SID...  22.3 us
    pallas_call x1, Pallas kernels, body(): pl.pallas_call(functools.partial(finish, rounds, total_slots), out_shape=...  0.67 us

profile of v6, /device:TPU:1, one launch (start us, length us, event | category | flops | bytes accessed | tf_op | source)
XLA Modules:
  0.0 23.6 jit_solution(17107035764192135986)
XLA Ops:
  0.6 22.3 %shard_map.76.sums_ref = f32[16,128]{1,0:T(8,128)S(1)} custom-call(f32[3,64,128]{2,1,0:T(8,128)} %bitcast.8, f32[3,64,128]{2,1,0:T(8,128)} %bitcast.9, s32[8,8]{1,0:T(8,128)} %bitcast.11, s32[8,8,128]{2,1,0:T(8,128)} %bitcast.10, s32[1,8]{1,0:T(1,128)} %bitcast.12), custom_call_target="tpu_custom_call" | custom-call | tf_op jit(solution)/shard_map/pallas_call | solution.py:309
  22.9 0.7 %shard_map.77 = (f32[1,36]{1,0:T(1,128)}, f32[1,6]{1,0:T(1,128)}, f32[8,36]{1,0:T(8,128)}) custom-call(f32[16,128]{1,0:T(8,128)S(1)} %shard_map.76.sums_ref), custom_call_target="tpu_custom_call" | custom-call | tf_op jit(solution)/shard_map/pallas_call | solution.py:341
